TPU v7x, 32 devices: a whole 2x2x4 slice. The times are simulated.
32 devices in a mesh: fsdp: 8 (over z, x), dp: 4 (over y, core).
Axes of the slice: x: 2, y: 2, z: 4, core: 2. Of those that a mesh axis runs over, the one named last changes fastest.
Arguments:
- inputs: bfloat16 [32768, 768], P(('fsdp', 'dp')), may hold values from -6 to 6
- row_ids: int32 [32768], P(('fsdp', 'dp')), may hold values from 0 to 7, as said below
- ln_gains: bfloat16 [2, 768], P(None, 'fsdp'), may hold values from 0.099609375 to 1.8984375
- biases: bfloat16 [6, 768], P(None, 'fsdp'), may hold values from -3 to 3
- w_qkv: bfloat16 [768, 2304], P('fsdp'), may hold values from -0.21875 to 0.21875
- w_out: bfloat16 [768, 768], P('fsdp'), may hold values from -0.75 to 0.75
- w_up: bfloat16 [768, 3072], P('fsdp'), may hold values from -0.21875 to 0.21875
- bias_up: bfloat16 [3072], P('fsdp'), may hold values from -3 to 3
- w_down: bfloat16 [3072, 768], P('fsdp'), may hold values from -0.109375 to 0.109375
- cotangent: bfloat16 [32768, 768], P(('fsdp', 'dp')), may hold values from -6 to 6
Outputs:
- block_out: bfloat16 [32768, 768], P(('fsdp', 'dp'))
- d_inputs: float32 [32768, 768], P(('fsdp', 'dp'))
- g_ln_gains: float32 [2, 768], P(None, 'fsdp')
- g_biases: float32 [6, 768], P(None, 'fsdp')
- g_w_qkv: float32 [768, 2304], P('fsdp')
- g_w_out: float32 [768, 768], P('fsdp')
- g_w_up: float32 [768, 3072], P('fsdp')
- g_bias_up: float32 [3072], P('fsdp')
- g_w_down: float32 [3072, 768], P('fsdp')
Inputs may be any that keep to these rules, and one draw needn't show every extreme that they name: `row_ids`: on each device the 1024 tokens form rows of 128 or 256 consecutive tokens, the longer rows first, so that each row starts at a multiple of its own length; the value numbers a token's row on its device from 0 in order; some device holds only rows of 128.
All inputs are finite; a program needn't handle non-finite values.
Results may differ from a plain program's by a relative error of at most 0.011.
Values may be sent and summed in bfloat16 or wider, within the bound.
A program may use at most 256 MiB of HBM per device.

v0:
```python
import math
import jax
import jax.numpy as jnp
from jax import lax
from jax.sharding import PartitionSpec as P

HEADS = 12
HEAD = 64
BLOCK = 512
norm_eps = 1e-05


def layer_norm(values, gain, shift):
    center = values - jnp.mean(values, axis=-1, keepdims=True)
    spread = jnp.mean(center * center, axis=-1, keepdims=True)
    return center * lax.rsqrt(spread + norm_eps) * gain + shift


def gelu_tanh(values):
    inner = math.sqrt(2.0 / math.pi) * (values + 0.044715 * values * values * values)
    return 0.5 * values * (1.0 + jnp.tanh(inner))


def contract_rows(left, right):
    return lax.dot_general(
        left, right, (((0,), (0,)), ((), ())), preferred_element_type=jnp.float32
    )


def contract_cols(left, right):
    return lax.dot_general(
        left, right, (((1,), (1,)), ((), ())), preferred_element_type=jnp.float32
    )


def split_heads(values):
    return values.reshape(values.shape[0], HEADS, values.shape[1] // HEADS)


def block_scores(query, keys, query_rows, key_rows):
    raw_scores = jnp.einsum(
        "qhd,khd->hqk", split_heads(query), split_heads(keys), preferred_element_type=jnp.float32
    )
    raw_scores = raw_scores * (1.0 / math.sqrt(HEAD))
    same_row = (query_rows[:, None] == key_rows[None, :])[None]
    return jnp.where(same_row, raw_scores, -1000000000.0)


def attend_forward(query, keys, values, query_rows, key_rows):
    scores = block_scores(query, keys, query_rows, key_rows)
    row_max = jnp.max(scores, axis=-1, keepdims=True)
    exponent = jnp.exp(scores - row_max)
    row_sum = jnp.sum(exponent, axis=-1, keepdims=True)
    attn_probs = (exponent / row_sum).astype(jnp.bfloat16)
    result = jnp.einsum(
        "hqk,khd->qhd", attn_probs, split_heads(values), preferred_element_type=jnp.float32
    )
    return (result.reshape(query.shape[0], -1), (row_max + jnp.log(row_sum))[..., 0])


def attend_backward(query, keys, values, query_rows, key_rows, log_sums, grad_out):
    scores = block_scores(query, keys, query_rows, key_rows)
    attn_probs = jnp.exp(scores - log_sums[..., None])
    probs_low = attn_probs.astype(jnp.bfloat16)
    grad_heads = split_heads(grad_out)
    d_values = jnp.einsum("hqk,qhd->khd", probs_low, grad_heads, preferred_element_type=jnp.float32)
    d_probs = jnp.einsum(
        "qhd,khd->hqk", grad_heads, split_heads(values), preferred_element_type=jnp.float32
    )
    inner = jnp.sum(attn_probs * d_probs, axis=-1, keepdims=True)
    d_scores = (attn_probs * (d_probs - inner)).astype(jnp.bfloat16)
    scale = 1.0 / math.sqrt(HEAD)
    d_query = (
        jnp.einsum("hqk,khd->qhd", d_scores, split_heads(keys), preferred_element_type=jnp.float32)
        * scale
    )
    d_keys = (
        jnp.einsum("hqk,qhd->khd", d_scores, split_heads(query), preferred_element_type=jnp.float32)
        * scale
    )
    return (
        d_query.reshape(query.shape[0], -1),
        d_keys.reshape(keys.shape[0], -1),
        d_values.reshape(keys.shape[0], -1),
    )


def per_device(inputs, row_ids, ln_gains, biases, w_qkv, w_out, w_up, bias_up, w_down, cotangent):
    gathered = (
        lax.all_gather(ln_gains, "fsdp", axis=1, tiled=True),
        lax.all_gather(biases, "fsdp", axis=1, tiled=True),
        lax.all_gather(w_qkv, "fsdp", axis=0, tiled=True),
        lax.all_gather(w_out, "fsdp", axis=0, tiled=True),
        lax.all_gather(w_up, "fsdp", axis=0, tiled=True),
        lax.all_gather(bias_up, "fsdp", axis=0, tiled=True),
        lax.all_gather(w_down, "fsdp", axis=0, tiled=True),
    )
    gains = gathered[0].astype(jnp.float32)
    shifts = gathered[1].astype(jnp.float32)
    full_qkv, full_out, full_up, full_bias_up, full_down = (
        gathered[2],
        gathered[3],
        gathered[4],
        gathered[5],
        gathered[6],
    )
    width = full_out.shape[0]
    rows_n = inputs.shape[0]
    blocks_n = rows_n // BLOCK
    tokens_f = inputs.astype(jnp.float32)
    normed_f, norm_pull = jax.vjp(layer_norm, tokens_f, gains[0], shifts[0])
    normed = normed_f.astype(jnp.bfloat16)
    qkv_bias = jnp.concatenate([shifts[1], jnp.zeros_like(shifts[1]), shifts[2]])
    qkv = (jnp.dot(normed, full_qkv, preferred_element_type=jnp.float32) + qkv_bias).astype(
        jnp.bfloat16
    )
    query = qkv[:, :width]
    keys = qkv[:, width : 2 * width]
    values = qkv[:, 2 * width :]
    query_blocks = query.reshape(blocks_n, BLOCK, width)
    row_blocks = row_ids.reshape(blocks_n, BLOCK)

    def forward_block(entry):
        return attend_forward(entry[0], keys, values, entry[1], row_ids)

    mixed, log_sums = lax.map(forward_block, (query_blocks, row_blocks))
    mixed = mixed.reshape(rows_n, width).astype(jnp.bfloat16)
    middle = tokens_f + jnp.dot(mixed, full_out, preferred_element_type=jnp.float32) + shifts[3]
    normed_two_f, second_pull = jax.vjp(layer_norm, middle, gains[1], shifts[4])
    normed_two = normed_two_f.astype(jnp.bfloat16)
    upper = jnp.dot(normed_two, full_up, preferred_element_type=jnp.float32) + full_bias_up.astype(
        jnp.float32
    )
    hidden_f, gelu_pull = jax.vjp(gelu_tanh, upper)
    hidden = hidden_f.astype(jnp.bfloat16)
    block_out = (
        middle + jnp.dot(hidden, full_down, preferred_element_type=jnp.float32) + shifts[5]
    ).astype(jnp.bfloat16)
    again = (
        lax.all_gather(ln_gains, "fsdp", axis=1, tiled=True),
        lax.all_gather(biases, "fsdp", axis=1, tiled=True),
        lax.all_gather(w_qkv, "fsdp", axis=0, tiled=True),
        lax.all_gather(w_out, "fsdp", axis=0, tiled=True),
        lax.all_gather(w_up, "fsdp", axis=0, tiled=True),
        lax.all_gather(bias_up, "fsdp", axis=0, tiled=True),
        lax.all_gather(w_down, "fsdp", axis=0, tiled=True),
    )
    back_qkv, back_out, back_up, back_down = (again[2], again[3], again[4], again[6])
    grad_out = cotangent.astype(jnp.float32)
    grad_shift_down = jnp.sum(grad_out, axis=0)
    grad_down = contract_rows(hidden, cotangent)
    d_hidden = contract_cols(cotangent, back_down)
    d_up = gelu_pull(d_hidden)[0].astype(jnp.bfloat16)
    grad_up = contract_rows(normed_two, d_up)
    grad_bias_up = jnp.sum(d_up, axis=0, dtype=jnp.float32)
    d_normed_two = contract_cols(d_up, back_up)
    d_middle_norm, grad_gain_two, grad_shift_two = second_pull(d_normed_two)
    d_middle = grad_out + d_middle_norm
    grad_shift_out = jnp.sum(d_middle, axis=0)
    d_middle_low = d_middle.astype(jnp.bfloat16)
    grad_out_proj = contract_rows(mixed, d_middle_low)
    d_mixed = contract_cols(d_middle_low, back_out).astype(jnp.bfloat16)
    d_blocks = d_mixed.reshape(blocks_n, BLOCK, width)

    def backward_step(carry, entry):
        d_query, d_keys, d_values = attend_backward(
            entry[0], keys, values, entry[1], row_ids, entry[2], entry[3]
        )
        return ((carry[0] + d_keys, carry[1] + d_values), d_query)

    empty = jnp.zeros((rows_n, width), jnp.float32)
    (d_keys, d_values), d_query = lax.scan(
        backward_step, (empty, empty), (query_blocks, row_blocks, log_sums, d_blocks)
    )
    d_query = d_query.reshape(rows_n, width)
    d_qkv = jnp.concatenate([d_query, d_keys, d_values], axis=1).astype(jnp.bfloat16)
    grad_qkv = contract_rows(normed, d_qkv)
    grad_bias_query = jnp.sum(d_qkv[:, :width], axis=0, dtype=jnp.float32)
    grad_bias_value = jnp.sum(d_qkv[:, 2 * width :], axis=0, dtype=jnp.float32)
    d_normed = contract_cols(d_qkv, back_qkv)
    d_tokens_norm, grad_gain_one, grad_shift_one = norm_pull(d_normed)
    d_inputs = d_middle + d_tokens_norm
    grad_gains = jnp.stack([grad_gain_one, grad_gain_two])
    grad_shifts = jnp.stack(
        [
            grad_shift_one,
            grad_bias_query,
            grad_bias_value,
            grad_shift_out,
            grad_shift_two,
            grad_shift_down,
        ]
    )
    owned = (
        lax.psum_scatter(grad_gains, "fsdp", scatter_dimension=1, tiled=True),
        lax.psum_scatter(grad_shifts, "fsdp", scatter_dimension=1, tiled=True),
        lax.psum_scatter(grad_qkv, "fsdp", scatter_dimension=0, tiled=True),
        lax.psum_scatter(grad_out_proj, "fsdp", scatter_dimension=0, tiled=True),
        lax.psum_scatter(grad_up, "fsdp", scatter_dimension=0, tiled=True),
        lax.psum_scatter(grad_bias_up, "fsdp", scatter_dimension=0, tiled=True),
        lax.psum_scatter(grad_down, "fsdp", scatter_dimension=0, tiled=True),
    )
    summed = lax.psum((owned[0], owned[1], owned[2], owned[3], owned[4], owned[5], owned[6]), "dp")
    return (
        block_out,
        d_inputs,
        summed[0],
        summed[1],
        summed[2],
        summed[3],
        summed[4],
        summed[5],
        summed[6],
    )


def solution(mesh):
    placed = (
        P(("fsdp", "dp"), None),
        P(("fsdp", "dp")),
        P(None, "fsdp"),
        P(None, "fsdp"),
        P("fsdp", None),
        P("fsdp", None),
        P("fsdp", None),
        P("fsdp"),
        P("fsdp", None),
        P(("fsdp", "dp"), None),
    )
    return jax.shard_map(
        per_device,
        mesh=mesh,
        in_specs=placed,
        out_specs=(
            P(("fsdp", "dp"), None),
            P(("fsdp", "dp"), None),
            P(None, "fsdp"),
            P(None, "fsdp"),
            P("fsdp", None),
            P("fsdp", None),
            P("fsdp", None),
            P("fsdp"),
            P("fsdp", None),
        ),
        check_vma=False,
    )
```

profile of v0, /device:TPU:0, one launch (start us, length us, event | category | flops | bytes accessed | tf_op | source)
XLA Modules:
  0.0 1196.6 jit_solution(12556076253939985790)
XLA Ops:
  11.4 22.7 %all-gather = bf16[8,96,2]{1,2,0:T(2,128)(2,1)S(1)} all-gather(bf16[1,96,2]{1,2,0:T(2,128)(2,1)} %bitcast.158), channel_id=1, replica_groups=mesh['fsdp'=8,'dp'=4] {'fsdp'}, dimensions={0}, use_global_device_ids=true | all-gather | bytes 3456 | tf_op jit(solution)/shard_map/all_gather | solution.py:90
  34.9 26.7 %all-gather.2 = bf16[8,1,384]{2,1,0:T(2,128)(2,1)S(1)} all-gather(bf16[1,1,384]{2,1,0:T(2,128)(2,1)S(1)} %reshape.237), channel_id=1, replica_groups=mesh['fsdp'=8,'dp'=4] {'fsdp'}, dimensions={0}, use_global_device_ids=true | all-gather | bytes 6912 | tf_op jit(solution)/shard_map/all_gather | solution.py:95
  62.2 26.7 %all-gather.1 = bf16[8,96,6]{1,2,0:T(8,128)(2,1)S(1)} all-gather(bf16[1,96,6]{1,2,0:T(8,128)(2,1)} %bitcast.157), channel_id=1, replica_groups=mesh['fsdp'=8,'dp'=4] {'fsdp'}, dimensions={0}, use_global_device_ids=true | all-gather | bytes 10368 | tf_op jit(solution)/shard_map/all_gather | solution.py:91
  108.2 89.3 %while.27 = (s32[]{:T(128)}, bf16[2,512,768]{2,1,0:T(8,128)(2,1)}, f32[2,12,512]{2,1,0:T(8,128)S(1)}, s32[2,512]{1,0:T(2,128)S(1)}, s32[1024]{0:T(1024)S(1)}, /*...) while((s32[]{:T(128)}, bf16[2,512,768]{2,1,0:T(8,128)(2,1)}, ...), condition=%wide.region_5.6_spmd, body=%wide.region_2.5_spmd.sunk | while | flops 1686628352 | bytes 187926672 | solution.py:126
  120.3 12.8 %fusion.104 = f32[12,512]{1,0:T(8,128)S(1)} fusion(f32[12,512,1024]{2,1,0:T(8,128)} %get-tuple-element.454, f32[12,512]{1,0:T(8,128)S(1)} %get-tuple-element.455, pred[512,1024]{1,0:T(8,128)(4,1)S(1)} %broadcast_compare_fusion.4), kind=kLoop, calls=%fused_computation.4.clone.1 | loop fusion | flops 25159680 | bytes 25739264 | tf_op jit(solution)/shard_map/while/body/eval_jaxpr/reduce_sum | solution.py:53
  159.1 12.4 %fusion.104 = f32[12,512]{1,0:T(8,128)S(1)} fusion(f32[12,512,1024]{2,1,0:T(8,128)} %get-tuple-element.454, f32[12,512]{1,0:T(8,128)S(1)} %get-tuple-element.455, pred[512,1024]{1,0:T(8,128)(4,1)S(1)} %broadcast_compare_fusion.4), kind=kLoop, calls=%fused_computation.4.clone.1 | loop fusion | flops 25159680 | bytes 25739264 | tf_op jit(solution)/shard_map/while/body/eval_jaxpr/reduce_sum | solution.py:53
  214.7 65.3 %all-gather.14.cloned.1.call-done = bf16[3072,768]{1,0:T(8,128)(2,1)} async-done(((bf16[384,768]{1,0:T(8,128)(2,1)}), bf16[3072,768]{1,0:T(8,128)(2,1)}) %all-gather.14.cloned.1.call-update) | async-done | bytes 4718608 | tf_op jit(solution)/shard_map/all_gather | solution.py:96
  280.0 17.9 %convert_reduce_fusion = (f32[3072]{0:T(1024)}, bf16[1024,3072]{1,0:T(8,128)(2,1)S(1)}) fusion(f32[1024,3072]{1,0:T(8,128)} %fusion.43, f32[3072]{0:T(1024)S(1)} %bitcast.154, bf16[1024,768]{1,0:T(8,128)(2,1)S(1)} %copy-done.24, bf16[3072,768]{1,0:T(8,128)(2,1)} %all-gather.14.cloned.1.call-done), kind=kOutput, calls=%fused_computation.41 | convolution fusion | flops 4916769792 | bytes 25190400 | tf_op jit(solution)/shard_map/dot_general | solution.py:31
  324.8 179.8 %while.28 = (s32[]{:T(128)}, f32[1024,768]{0,1:T(8,128)}, f32[1024,768]{0,1:T(8,128)}, bf16[2,512,768]{2,1,0:T(8,128)(2,1)}, bf16[2,512,768]{1,2,0:T(8,128)(2,1)...) while((s32[]{:T(128)}, f32[1024,768]{0,1:T(8,128)}, ...), condition=%wide.region_12.13_spmd.clone, body=%wide.region_10.12_spmd.clone.sunk | while | flops 4126140416 | bytes 298764608 | solution.py:172
  339.4 13.3 %fusion.117 = f32[12,64,1024]{2,1,0:T(8,128)} fusion(bf16[512,12,64]{0,2,1:T(8,128)(2,1)S(1)} %bitcast.137, f32[12,512,1024]{2,1,0:T(8,128)} %fusion.116, f32[12,512]{1,0:T(8,128)S(1)} %dynamic-slice_bitcast_fusion.2, pred[512,1024]{1,0:T(8,128)(4,1)S(1)} %broadcast_compare_fusion.5), kind=kOutput, calls=%fused_computation.17.clone.1 | convolution fusion | flops 830472192 | bytes 29646848 | tf_op jit(solution)/shard_map/while/body/eval_jaxpr/hqk,qhd->khd/dot_general | solution.py:66
  352.7 18.1 %multiply_reduce_fusion.5 = (f32[12,512]{1,0:T(8,128)S(1)}, f32[12,512,1024]{2,1,0:T(8,128)}) fusion(f32[12,512,1024]{2,1,0:T(8,128)} %fusion.116, f32[12,512]{1,0:T(8,128)S(1)} %dynamic-slice_bitcast_fusion.2, pred[512,1024]{1,0:T(8,128)(4,1)S(1)} %broadcast_compare_fusion.5, bf16[512,12,64]{0,2,1:T(8,128)(2,1)} %bitcast.136, ...), kind=kOutput, calls=%fused_computation.14.clone.1 | convolution fusion | flops 836757504 | bytes 53264384 | tf_op jit(solution)/shard_map/while/body/eval_jaxpr/qhd,khd->hqk/dot_general | solution.py:67
  370.8 21.8 %multiply_convert_fusion.2 = bf16[12,512,1024]{2,1,0:T(8,128)(2,1)} fusion(f32[12,512,1024]{2,1,0:T(8,128)} %get-tuple-element.467, f32[12,512,1024]{2,1,0:T(8,128)} %fusion.116, f32[12,512]{1,0:T(8,128)S(1)} %get-tuple-element.468, f32[12,512]{1,0:T(8,128)S(1)} %dynamic-slice_bitcast_fusion.2, pred[512,1024]{1,0:T(8,128)(4,1)S(1)} %broadcast_compare_fusion.5), kind=kLoop, calls=%fused_computation.13.clone.1 | loop fusion | flops 37748736 | bytes 63488000 | tf_op jit(solution)/shard_map/while/body/eval_jaxpr/convert_element_type | solution.py:71
  429.4 13.0 %fusion.117 = f32[12,64,1024]{2,1,0:T(8,128)} fusion(bf16[512,12,64]{0,2,1:T(8,128)(2,1)S(1)} %bitcast.137, f32[12,512,1024]{2,1,0:T(8,128)} %fusion.116, f32[12,512]{1,0:T(8,128)S(1)} %dynamic-slice_bitcast_fusion.2, pred[512,1024]{1,0:T(8,128)(4,1)S(1)} %broadcast_compare_fusion.5), kind=kOutput, calls=%fused_computation.17.clone.1 | convolution fusion | flops 830472192 | bytes 29646848 | tf_op jit(solution)/shard_map/while/body/eval_jaxpr/hqk,qhd->khd/dot_general | solution.py:66
  442.4 18.1 %multiply_reduce_fusion.5 = (f32[12,512]{1,0:T(8,128)S(1)}, f32[12,512,1024]{2,1,0:T(8,128)}) fusion(f32[12,512,1024]{2,1,0:T(8,128)} %fusion.116, f32[12,512]{1,0:T(8,128)S(1)} %dynamic-slice_bitcast_fusion.2, pred[512,1024]{1,0:T(8,128)(4,1)S(1)} %broadcast_compare_fusion.5, bf16[512,12,64]{0,2,1:T(8,128)(2,1)} %bitcast.136, ...), kind=kOutput, calls=%fused_computation.14.clone.1 | convolution fusion | flops 836757504 | bytes 53264384 | tf_op jit(solution)/shard_map/while/body/eval_jaxpr/qhd,khd->hqk/dot_general | solution.py:67
  460.5 21.2 %multiply_convert_fusion.2 = bf16[12,512,1024]{2,1,0:T(8,128)(2,1)} fusion(f32[12,512,1024]{2,1,0:T(8,128)} %get-tuple-element.467, f32[12,512,1024]{2,1,0:T(8,128)} %fusion.116, f32[12,512]{1,0:T(8,128)S(1)} %get-tuple-element.468, f32[12,512]{1,0:T(8,128)S(1)} %dynamic-slice_bitcast_fusion.2, pred[512,1024]{1,0:T(8,128)(4,1)S(1)} %broadcast_compare_fusion.5), kind=kLoop, calls=%fused_computation.13.clone.1 | loop fusion | flops 37748736 | bytes 63488000 | tf_op jit(solution)/shard_map/while/body/eval_jaxpr/convert_element_type | solution.py:71
  520.8 12.9 %fusion.44 = f32[3072,768]{1,0:T(8,128)} fusion(bf16[1024,768]{1,0:T(8,128)(2,1)S(1)} %copy-done.25, f32[1024,3072]{1,0:T(8,128)} %fusion.43, f32[3072]{0:T(1024)S(1)} %bitcast.155), kind=kOutput, calls=%fused_computation.105 | convolution fusion | flops 4863295488 | bytes 23605248 | tf_op jit(solution)/shard_map/dot_general | solution.py:25
  577.7 69.8 %reduce-scatter.11.cloned.1.call-done = f32[96,2304]{1,0:T(8,128)} async-done(((f32[768,2304]{1,0:T(8,128)}), f32[96,2304]{1,0:T(8,128)}) %reduce-scatter.11.cloned.1.call-update) | async-done | bytes 884752 | tf_op jit(solution)/shard_map/reduce_scatter | solution.py:197
  647.5 164.9 %reduce-scatter.17.cloned.1.call-done = f32[384,768]{1,0:T(8,128)} async-done(((f32[3072,768]{1,0:T(8,128)}), f32[384,768]{1,0:T(8,128)}) %reduce-scatter.17.cloned.1.call-update) | async-done | bytes 1179664 | tf_op jit(solution)/shard_map/reduce_scatter | solution.py:201
  812.3 164.8 %reduce-scatter.15.cloned.1.call-done = f32[96,3072]{1,0:T(8,128)} async-done(((f32[768,3072]{1,0:T(8,128)}), f32[96,3072]{1,0:T(8,128)}) %reduce-scatter.15.cloned.1.call-update) | async-done | bytes 1179664 | tf_op jit(solution)/shard_map/reduce_scatter | solution.py:199
  977.2 11.5 add_convert_fusion.1
  993.8 35.2 %all-reduce = f32[3072]{0:T(1024)S(1)} all-reduce(f32[3072]{0:T(1024)S(1)} %copy-done.51), channel_id=7, replica_groups=mesh['fsdp'=8,'dp'=4] {'fsdp'}, use_global_device_ids=true, to_apply=%region_34.35.clone | all-reduce | flops 3072 | bytes 24576
  1029.1 13.3 %reduce-scatter.19.cloned.1.call-done = f32[96,2]{1,0:T(8,128)} async-done(((f32[768,2]{1,0:T(8,128)}), f32[96,2]{1,0:T(8,128)}) %reduce-scatter.19.cloned.1.call-update) | async-done | bytes 784
  1043.2 64.1 %reduce-scatter.21.cloned.1.call-done = f32[96,6]{1,0:T(8,128)} async-done(((f32[768,6]{1,0:T(8,128)}), f32[96,6]{1,0:T(8,128)}) %reduce-scatter.21.cloned.1.call-update) | async-done | bytes 2320
  1114.5 69.3 %all-reduce.5.cloned.1.call-done = (f32[96,2304]{1,0:T(8,128)}, f32[96,768]{1,0:T(8,128)}, f32[96,3072]{1,0:T(8,128)}, f32[384,768]{1,0:T(8,128)}) async-done(((f32[96,2304]{1,0:T(8,128)}, f32[96,768]{1,0:T(8,128)}, f32[96,3072]{1,0:T(8,128)}, f32[384,768]{1,0:T(8,128)}), (f32[96,2304]{1,0:T(8,128)}, f32[96,768]{1,0:T(8,128)}, f32[96,3072]{1,0:T(8,128)}, f32[384,768]{1,0:T(8,128)})) %all-reduce.5.cloned.1.call-update) | async-done | bytes 3538960 | tf_op jit(solution)/shard_map/psum | solution.py:203
  (275 shorter events, 272.0 us)
Async XLA Ops:
  7.2 86.7 %all-gather.8.cloned.1.call-start = ((), (), s32[]{:S(2)}) async-start(), calls=%async_computation.6 | async-start | bytes 3981312 | tf_op jit(solution)/shard_map/all_gather | solution.py:92
  7.9 189.5 %all-gather.10.cloned.1.call-start = ((), (), s32[]{:S(2)}) async-start(), calls=%async_computation.7 | async-start | bytes 1327104 | tf_op jit(solution)/shard_map/all_gather | solution.py:93
  8.7 194.8 %all-gather.12.cloned.1.call-start = ((), (), s32[]{:S(2)}) async-start(), calls=%async_computation.8 | async-start | bytes 5308416 | tf_op jit(solution)/shard_map/all_gather | solution.py:94
  9.4 270.6 %all-gather.14.cloned.1.call-start = ((), (), s32[]{:S(2)}) async-start(), calls=%async_computation.9 | async-start | bytes 5308416 | tf_op jit(solution)/shard_map/all_gather | solution.py:96
  10.0 567.7 %reduce-scatter.13.cloned.1.call-start = ((), (), s32[]{:S(2)}) async-start(), calls=%async_computation.11 | async-start | bytes 2654208 | tf_op jit(solution)/shard_map/reduce_scatter | solution.py:198
  34.9 59.1 %copy-start.40 = (f32[768]{0:T(1024)}, f32[768]{0:T(1024)S(1)}, u32[]{:S(2)}) copy-start(f32[768]{0:T(1024)S(1)} %get-tuple-element.277) | copy-start | bytes 9220
  108.1 89.3 %copy-start.56 = (f32[768]{0:T(1024)S(1)}, f32[768]{0:T(1024)}, u32[]{:S(2)}) copy-start(f32[768]{0:T(1024)} %get-tuple-element.272) | copy-start | bytes 9220
  120.3 16.0 %copy-start = (f32[12,512,1024]{2,1,0:T(8,128)S(1)}, f32[12,512,1024]{2,1,0:T(8,128)}, u32[]{:S(2)}) copy-start(f32[12,512,1024]{2,1,0:T(8,128)} %get-tuple-element.454) | copy-start | bytes 75497472 | tf_op jit(solution)/shard_map/while
  159.1 15.5 %copy-start = (f32[12,512,1024]{2,1,0:T(8,128)S(1)}, f32[12,512,1024]{2,1,0:T(8,128)}, u32[]{:S(2)}) copy-start(f32[12,512,1024]{2,1,0:T(8,128)} %get-tuple-element.454) | copy-start | bytes 75497472 | tf_op jit(solution)/shard_map/while
  201.4 111.9 %copy-start.29 = (f32[1024]{0:T(1024)}, f32[1024]{0:T(1024)S(1)}, u32[]{:S(2)}) copy-start(f32[1024]{0:T(1024)S(1)} %broadcast_multiply_fusion) | copy-start | bytes 12292
  203.5 109.8 %copy-start.34 = (f32[1024]{0:T(1024)}, f32[1024]{0:T(1024)S(1)}, u32[]{:S(2)}) copy-start(f32[1024]{0:T(1024)S(1)} %fusion.37) | copy-start | bytes 12292
  203.5 76.5 %copy-start.24 = (bf16[1024,768]{1,0:T(8,128)(2,1)S(1)}, bf16[1024,768]{1,0:T(8,128)(2,1)}, u32[]{:S(2)}) copy-start(bf16[1024,768]{1,0:T(8,128)(2,1)} %param.23) | copy-start | bytes 4718596
  203.5 76.5 %copy-start.49 = (f32[8,1,384]{2,1,0:T(1,128)S(1)}, f32[8,1,384]{2,1,0:T(1,128)}, u32[]{:S(2)}) copy-start(f32[8,1,384]{2,1,0:T(1,128)} %convert_element_type.84) | copy-start | bytes 36868
  280.0 17.9 %copy-start.22 = (bf16[768,3072]{1,0:T(8,128)(2,1)S(1)}, bf16[768,3072]{1,0:T(8,128)(2,1)}, u32[]{:S(2)}) copy-start(bf16[768,3072]{1,0:T(8,128)(2,1)} %all-gather.12.cloned.1.call-done) | copy-start | bytes 14155780
  319.6 327.8 %reduce-scatter.11.cloned.1.call-start = ((), (), s32[]{:S(2)}) async-start(), calls=%async_computation.10 | async-start | bytes 7962624 | tf_op jit(solution)/shard_map/reduce_scatter | solution.py:197
  329.1 10.3 copy-start.7
  419.3 10.1 copy-start.7
  519.4 293.0 %reduce-scatter.17.cloned.1.call-start = ((), (), s32[]{:S(2)}) async-start(), calls=%async_computation.13 | async-start | bytes 10616832 | tf_op jit(solution)/shard_map/reduce_scatter | solution.py:201
  533.7 443.5 %reduce-scatter.15.cloned.1.call-start = ((), (), s32[]{:S(2)}) async-start(), calls=%async_computation.12 | async-start | bytes 10616832 | tf_op jit(solution)/shard_map/reduce_scatter | solution.py:199
  546.1 496.3 %reduce-scatter.19.cloned.1.call-start = ((), (), s32[]{:S(2)}) async-start(), calls=%async_computation.14 | async-start | bytes 442368
  573.3 403.9 %copy-start.13 = (f32[1024,768]{0,1:T(8,128)S(1)}, f32[1024,768]{0,1:T(8,128)}, u32[]{:S(2)}) copy-start(f32[1024,768]{0,1:T(8,128)} %copy-done.10) | copy-start | bytes 9437188
  573.3 403.9 %copy-start.53 = (f32[768]{0:T(1024)S(1)}, f32[768]{0:T(1024)}, u32[]{:S(2)}) copy-start(f32[768]{0:T(1024)} %get-tuple-element.271) | copy-start | bytes 9220
  573.4 533.9 %reduce-scatter.21.cloned.1.call-start = ((), (), s32[]{:S(2)}) async-start(), calls=%async_computation.15 | async-start | bytes 442368
  576.3 607.5 %all-reduce.5.cloned.1.call-start = ((), (), s32[]{:S(2)}) async-start(), calls=%async_computation.16 | async-start | bytes 7077888 | tf_op jit(solution)/shard_map/psum | solution.py:203
  (53 other events, 191.7 us)
Sparse Core Ops, SparseCore 0:
  10.2 67.5 all-gather.7
  79.9 40.0 all-gather.9
  122.2 78.0 all-gather.11
  202.3 77.6 all-gather.13
  319.8 67.9 reduce-scatter.12
  519.5 127.9 reduce-scatter.10
  651.1 161.2 reduce-scatter.16
  815.9 161.1 reduce-scatter.14
  981.0 61.2 reduce-scatter.18
  1046.0 61.2 reduce-scatter.20
  1109.9 73.8 all-reduce.4
where the time goes:
time: 1210 us; the launch traced here: 1200 us
  waiting for transfers between devices  614 us (51%)
  matrix products  259 us (21%)
  blocking collectives  118 us (10%)
  other arithmetic  95.8 us (8%)
  local copies, waits for them, and re-layouts  80.1 us (7%)
  between operations  15.3 us (1%)
  loops' own time  13.4 us (1%)
    reduce_scatter x1, waiting for transfers between devices, per_device(): lax.psum_scatter(grad_down, 'fsdp', scatter_dimension=0, tiled=True)  165 us
    reduce_scatter x1, waiting for transfers between devices, per_device(): lax.psum_scatter(grad_up, 'fsdp', scatter_dimension=0, tiled=True)  165 us
    unnamed x13, waiting for transfers between devices  80 us
    reduce_scatter x1, waiting for transfers between devices, per_device(): lax.psum_scatter(grad_qkv, 'fsdp', scatter_dimension=0, tiled=True)  69.8 us
    psum x1, waiting for transfers between devices, per_device(): lax.psum((owned[0], owned[1], owned[2], owned[3], owned[4], owned[5], own...  69.3 us
    all_gather x1, waiting for transfers between devices, per_device(): lax.all_gather(w_down, 'fsdp', axis=0, tiled=True)  65.3 us
    convert_element_type x2, other arithmetic, attend_backward(): d_scores = (attn_probs * (d_probs - inner)).astype(jnp.bfloat16)  43 us
    dot_general x4, matrix products, block_scores(): jnp.einsum('qhd,khd->hqk', split_heads(query), split_heads(keys), preferr...  41.9 us
  transfers between devices with their start and end apart: 11, of which 7 were waited for; matrix products, arithmetic and copies ran while one was open for 31% of the time, Pallas kernels for 0%

commit v1 on v0

--- a/solution.py
+++ b/solution.py
@@ -8,6 +8,18 @@
 HEAD = 64
 BLOCK = 512
 norm_eps = 1e-05
+
+
+def collect(array, axis, dim):
+    ways, here, step = (lax.axis_size(axis), lax.axis_index(axis), array.shape[dim])
+    line, have = (array, 1)
+    while have < ways:
+        line = jnp.concatenate(
+            [line, lax.ppermute(line, axis, [(d, (d - have) % ways) for d in range(ways)])],
+            axis=dim,
+        )
+        have = 2 * have
+    return jnp.roll(line, here * step, axis=dim)
 
 
 def layer_norm(values, gain, shift):
@@ -92,7 +104,7 @@
         lax.all_gather(w_qkv, "fsdp", axis=0, tiled=True),
         lax.all_gather(w_out, "fsdp", axis=0, tiled=True),
         lax.all_gather(w_up, "fsdp", axis=0, tiled=True),
-        lax.all_gather(bias_up, "fsdp", axis=0, tiled=True),
+        collect(bias_up, "fsdp", 0),
         lax.all_gather(w_down, "fsdp", axis=0, tiled=True),
     )
     gains = gathered[0].astype(jnp.float32)

time: 1210 us -> 1200 us (level)
  waiting for transfers between devices: 614 us -> 652 us
  blocking collectives: 118 us -> 85.8 us
  loops' own time: 13.4 us -> 1.29 us
    all_gather x1 -> x0, blocking collectives: 26.7 us -> none  [per_device(): lax.all_gather(bias_up, 'fsdp', axis=0, tiled=True)]
    all_gather x1, waiting for transfers between devices: 0.02 us -> 25.2 us  [per_device(): lax.all_gather(w_up, 'fsdp', axis=0, tiled=True)]
    another operation x1, loops' own time: 12.7 us -> 0.54 us  [per_device(): mixed, log_sums = lax.map(forward_block, (query_blocks, row_blocks))]
    unnamed x119 -> x127, local copies, waits for them, and re-layouts: 28.5 us -> 29.3 us
  transfers between devices with their start and end apart: 11 -> 14, of which waited for: 7 -> 11; matrix products, arithmetic and copies ran while one was open for 31% -> 31% of each run, Pallas kernels for 0% -> 0%
where the time goes in v1:
time: 1200 us
  waiting for transfers between devices  652 us (54%)
  matrix products  259 us (22%)
  other arithmetic  95.5 us (8%)
  blocking collectives  85.8 us (7%)
  local copies, waits for them, and re-layouts  80.9 us (7%)
  between operations  15.4 us (1%)
    reduce_scatter x1, waiting for transfers between devices, per_device(): lax.psum_scatter(grad_down, 'fsdp', scatter_dimension=0, tiled=True)  165 us
    reduce_scatter x1, waiting for transfers between devices, per_device(): lax.psum_scatter(grad_up, 'fsdp', scatter_dimension=0, tiled=True)  165 us
    unnamed x13, waiting for transfers between devices  79.5 us
    reduce_scatter x1, waiting for transfers between devices, per_device(): lax.psum_scatter(grad_qkv, 'fsdp', scatter_dimension=0, tiled=True)  69.8 us
    psum x1, waiting for transfers between devices, per_device(): lax.psum((owned[0], owned[1], owned[2], owned[3], owned[4], owned[5], own...  69.4 us
    all_gather x1, waiting for transfers between devices, per_device(): lax.all_gather(w_down, 'fsdp', axis=0, tiled=True)  68.6 us
    convert_element_type x2, other arithmetic, attend_backward(): d_scores = (attn_probs * (d_probs - inner)).astype(jnp.bfloat16)  43 us
    dot_general x4, matrix products, block_scores(): jnp.einsum('qhd,khd->hqk', split_heads(query), split_heads(keys), preferr...  41.7 us
  transfers between devices with their start and end apart: 14, of which 11 were waited for; matrix products, arithmetic and copies ran while one was open for 31% of the time, Pallas kernels for 0%

profile of v1, /device:TPU:0, one launch (start us, length us, event | category | flops | bytes accessed | tf_op | source)
XLA Modules:
  0.0 1196.8 jit_solution(8009775883081099555)
XLA Ops:
  15.6 17.3 %all-gather = bf16[8,96,2]{1,2,0:T(2,128)(2,1)S(1)} all-gather(bf16[1,96,2]{1,2,0:T(2,128)(2,1)} %bitcast.154), channel_id=1, replica_groups=mesh['fsdp'=8,'dp'=4] {'fsdp'}, dimensions={0}, use_global_device_ids=true | all-gather | bytes 3456 | tf_op jit(solution)/shard_map/all_gather | solution.py:102
  32.8 27.1 %all-gather.1 = bf16[8,96,6]{1,2,0:T(8,128)(2,1)S(1)} all-gather(bf16[1,96,6]{1,2,0:T(8,128)(2,1)} %bitcast.153), channel_id=1, replica_groups=mesh['fsdp'=8,'dp'=4] {'fsdp'}, dimensions={0}, use_global_device_ids=true | all-gather | bytes 10368 | tf_op jit(solution)/shard_map/all_gather | solution.py:103
  91.9 77.0 %while.27 = (s32[]{:T(128)}, bf16[2,512,768]{2,1,0:T(8,128)(2,1)}, f32[2,12,512]{2,1,0:T(8,128)S(1)}, s32[2,512]{1,0:T(2,128)S(1)}, s32[1024]{0:T(1024)S(1)}, /*...) while((s32[]{:T(128)}, bf16[2,512,768]{2,1,0:T(8,128)(2,1)}, ...), condition=%wide.region_5.6_spmd, body=%wide.region_2.5_spmd.sunk | while | flops 1686628352 | bytes 187926672 | solution.py:138
  104.7 12.4 %fusion.104 = f32[12,512]{1,0:T(8,128)S(1)} fusion(f32[12,512,1024]{2,1,0:T(8,128)} %get-tuple-element.454, f32[12,512]{1,0:T(8,128)S(1)} %get-tuple-element.455, pred[512,1024]{1,0:T(8,128)(4,1)S(1)} %broadcast_compare_fusion.4), kind=kLoop, calls=%fused_computation.4.clone.1 | loop fusion | flops 25159680 | bytes 25739264 | tf_op jit(solution)/shard_map/while/body/eval_jaxpr/reduce_sum | solution.py:65
  142.7 12.3 %fusion.104 = f32[12,512]{1,0:T(8,128)S(1)} fusion(f32[12,512,1024]{2,1,0:T(8,128)} %get-tuple-element.454, f32[12,512]{1,0:T(8,128)S(1)} %get-tuple-element.455, pred[512,1024]{1,0:T(8,128)(4,1)S(1)} %broadcast_compare_fusion.4), kind=kLoop, calls=%fused_computation.4.clone.1 | loop fusion | flops 25159680 | bytes 25739264 | tf_op jit(solution)/shard_map/while/body/eval_jaxpr/reduce_sum | solution.py:65
  174.9 25.2 %all-gather.11.cloned.1.call-done = bf16[768,3072]{1,0:T(8,128)(2,1)} async-done(((bf16[96,3072]{1,0:T(8,128)(2,1)}), bf16[768,3072]{1,0:T(8,128)(2,1)}) %all-gather.11.cloned.1.call-update) | async-done | bytes 4718608 | tf_op jit(solution)/shard_map/all_gather | solution.py:106
  211.3 68.6 %all-gather.13.cloned.1.call-done = bf16[3072,768]{1,0:T(8,128)(2,1)} async-done(((bf16[384,768]{1,0:T(8,128)(2,1)}), bf16[3072,768]{1,0:T(8,128)(2,1)}) %all-gather.13.cloned.1.call-update) | async-done | bytes 4718608 | tf_op jit(solution)/shard_map/all_gather | solution.py:108
  279.9 18.1 %convert_reduce_fusion = (f32[3072]{0:T(1024)}, bf16[1024,3072]{1,0:T(8,128)(2,1)S(1)}) fusion(f32[1024,3072]{1,0:T(8,128)} %fusion.43, f32[3072]{0:T(1024)S(1)} %copy-done.50, bf16[1024,768]{1,0:T(8,128)(2,1)S(1)} %copy-done.24, bf16[3072,768]{1,0:T(8,128)(2,1)} %all-gather.13.cloned.1.call-done), kind=kOutput, calls=%fused_computation.41 | convolution fusion | flops 4916769792 | bytes 25190400 | tf_op jit(solution)/shard_map/dot_general | solution.py:43
  324.9 179.8 %while.28 = (s32[]{:T(128)}, f32[1024,768]{0,1:T(8,128)}, f32[1024,768]{0,1:T(8,128)}, bf16[2,512,768]{2,1,0:T(8,128)(2,1)}, bf16[2,512,768]{1,2,0:T(8,128)(2,1)...) while((s32[]{:T(128)}, f32[1024,768]{0,1:T(8,128)}, ...), condition=%wide.region_12.13_spmd.clone, body=%wide.region_10.12_spmd.clone.sunk | while | flops 4126140416 | bytes 298764608 | solution.py:184
  339.5 13.3 %fusion.117 = f32[12,64,1024]{2,1,0:T(8,128)} fusion(bf16[512,12,64]{0,2,1:T(8,128)(2,1)S(1)} %bitcast.136, f32[12,512,1024]{2,1,0:T(8,128)} %fusion.116, f32[12,512]{1,0:T(8,128)S(1)} %dynamic-slice_bitcast_fusion.2, pred[512,1024]{1,0:T(8,128)(4,1)S(1)} %broadcast_compare_fusion.5), kind=kOutput, calls=%fused_computation.17.clone.1 | convolution fusion | flops 830472192 | bytes 29646848 | tf_op jit(solution)/shard_map/while/body/eval_jaxpr/hqk,qhd->khd/dot_general | solution.py:78
  352.8 18.1 %multiply_reduce_fusion.5 = (f32[12,512]{1,0:T(8,128)S(1)}, f32[12,512,1024]{2,1,0:T(8,128)}) fusion(f32[12,512,1024]{2,1,0:T(8,128)} %fusion.116, f32[12,512]{1,0:T(8,128)S(1)} %dynamic-slice_bitcast_fusion.2, pred[512,1024]{1,0:T(8,128)(4,1)S(1)} %broadcast_compare_fusion.5, bf16[512,12,64]{0,2,1:T(8,128)(2,1)} %bitcast.135, ...), kind=kOutput, calls=%fused_computation.14.clone.1 | convolution fusion | flops 836757504 | bytes 53264384 | tf_op jit(solution)/shard_map/while/body/eval_jaxpr/qhd,khd->hqk/dot_general | solution.py:79
  370.9 21.8 %multiply_convert_fusion.2 = bf16[12,512,1024]{2,1,0:T(8,128)(2,1)} fusion(f32[12,512,1024]{2,1,0:T(8,128)} %get-tuple-element.467, f32[12,512,1024]{2,1,0:T(8,128)} %fusion.116, f32[12,512]{1,0:T(8,128)S(1)} %get-tuple-element.468, f32[12,512]{1,0:T(8,128)S(1)} %dynamic-slice_bitcast_fusion.2, pred[512,1024]{1,0:T(8,128)(4,1)S(1)} %broadcast_compare_fusion.5), kind=kLoop, calls=%fused_computation.13.clone.1 | loop fusion | flops 37748736 | bytes 63488000 | tf_op jit(solution)/shard_map/while/body/eval_jaxpr/convert_element_type | solution.py:83
  429.5 13.0 %fusion.117 = f32[12,64,1024]{2,1,0:T(8,128)} fusion(bf16[512,12,64]{0,2,1:T(8,128)(2,1)S(1)} %bitcast.136, f32[12,512,1024]{2,1,0:T(8,128)} %fusion.116, f32[12,512]{1,0:T(8,128)S(1)} %dynamic-slice_bitcast_fusion.2, pred[512,1024]{1,0:T(8,128)(4,1)S(1)} %broadcast_compare_fusion.5), kind=kOutput, calls=%fused_computation.17.clone.1 | convolution fusion | flops 830472192 | bytes 29646848 | tf_op jit(solution)/shard_map/while/body/eval_jaxpr/hqk,qhd->khd/dot_general | solution.py:78
  442.5 18.1 %multiply_reduce_fusion.5 = (f32[12,512]{1,0:T(8,128)S(1)}, f32[12,512,1024]{2,1,0:T(8,128)}) fusion(f32[12,512,1024]{2,1,0:T(8,128)} %fusion.116, f32[12,512]{1,0:T(8,128)S(1)} %dynamic-slice_bitcast_fusion.2, pred[512,1024]{1,0:T(8,128)(4,1)S(1)} %broadcast_compare_fusion.5, bf16[512,12,64]{0,2,1:T(8,128)(2,1)} %bitcast.135, ...), kind=kOutput, calls=%fused_computation.14.clone.1 | convolution fusion | flops 836757504 | bytes 53264384 | tf_op jit(solution)/shard_map/while/body/eval_jaxpr/qhd,khd->hqk/dot_general | solution.py:79
  460.5 21.2 %multiply_convert_fusion.2 = bf16[12,512,1024]{2,1,0:T(8,128)(2,1)} fusion(f32[12,512,1024]{2,1,0:T(8,128)} %get-tuple-element.467, f32[12,512,1024]{2,1,0:T(8,128)} %fusion.116, f32[12,512]{1,0:T(8,128)S(1)} %get-tuple-element.468, f32[12,512]{1,0:T(8,128)S(1)} %dynamic-slice_bitcast_fusion.2, pred[512,1024]{1,0:T(8,128)(4,1)S(1)} %broadcast_compare_fusion.5), kind=kLoop, calls=%fused_computation.13.clone.1 | loop fusion | flops 37748736 | bytes 63488000 | tf_op jit(solution)/shard_map/while/body/eval_jaxpr/convert_element_type | solution.py:83
  520.9 12.9 %fusion.44 = f32[3072,768]{1,0:T(8,128)} fusion(bf16[1024,768]{1,0:T(8,128)(2,1)S(1)} %copy-done.25, f32[1024,3072]{1,0:T(8,128)} %fusion.43, f32[3072]{0:T(1024)S(1)} %copy-done.51), kind=kOutput, calls=%fused_computation.108 | convolution fusion | flops 4863295488 | bytes 23605248 | tf_op jit(solution)/shard_map/dot_general | solution.py:37
  577.8 69.8 %reduce-scatter.11.cloned.1.call-done = f32[96,2304]{1,0:T(8,128)} async-done(((f32[768,2304]{1,0:T(8,128)}), f32[96,2304]{1,0:T(8,128)}) %reduce-scatter.11.cloned.1.call-update) | async-done | bytes 884752 | tf_op jit(solution)/shard_map/reduce_scatter | solution.py:209
  647.6 164.9 %reduce-scatter.17.cloned.1.call-done = f32[384,768]{1,0:T(8,128)} async-done(((f32[3072,768]{1,0:T(8,128)}), f32[384,768]{1,0:T(8,128)}) %reduce-scatter.17.cloned.1.call-update) | async-done | bytes 1179664 | tf_op jit(solution)/shard_map/reduce_scatter | solution.py:213
  812.5 164.9 %reduce-scatter.15.cloned.1.call-done = f32[96,3072]{1,0:T(8,128)} async-done(((f32[768,3072]{1,0:T(8,128)}), f32[96,3072]{1,0:T(8,128)}) %reduce-scatter.15.cloned.1.call-update) | async-done | bytes 1179664 | tf_op jit(solution)/shard_map/reduce_scatter | solution.py:211
  977.4 11.5 add_convert_fusion.1
  994.0 35.2 %all-reduce = f32[3072]{0:T(1024)S(1)} all-reduce(f32[3072]{0:T(1024)S(1)} %copy-done.52), channel_id=7, replica_groups=mesh['fsdp'=8,'dp'=4] {'fsdp'}, use_global_device_ids=true, to_apply=%region_34.35.clone | all-reduce | flops 3072 | bytes 24576
  1029.3 13.2 %reduce-scatter.19.cloned.1.call-done = f32[96,2]{1,0:T(8,128)} async-done(((f32[768,2]{1,0:T(8,128)}), f32[96,2]{1,0:T(8,128)}) %reduce-scatter.19.cloned.1.call-update) | async-done | bytes 784
  1043.4 64.1 %reduce-scatter.21.cloned.1.call-done = f32[96,6]{1,0:T(8,128)} async-done(((f32[768,6]{1,0:T(8,128)}), f32[96,6]{1,0:T(8,128)}) %reduce-scatter.21.cloned.1.call-update) | async-done | bytes 2320
  1114.6 69.4 %all-reduce.5.cloned.1.call-done = (f32[96,2304]{1,0:T(8,128)}, f32[96,768]{1,0:T(8,128)}, f32[96,3072]{1,0:T(8,128)}, f32[384,768]{1,0:T(8,128)}) async-done(((f32[96,2304]{1,0:T(8,128)}, f32[96,768]{1,0:T(8,128)}, f32[96,3072]{1,0:T(8,128)}, f32[384,768]{1,0:T(8,128)}), (f32[96,2304]{1,0:T(8,128)}, f32[96,768]{1,0:T(8,128)}, f32[96,3072]{1,0:T(8,128)}, f32[384,768]{1,0:T(8,128)})) %all-reduce.5.cloned.1.call-update) | async-done | bytes 3538960 | tf_op jit(solution)/shard_map/psum | solution.py:215
  (292 shorter events, 288.0 us)
Async XLA Ops:
  7.2 70.7 %all-gather.7.cloned.1.call-start = ((), (), s32[]{:S(2)}) async-start(), calls=%async_computation.6 | async-start | bytes 3981312 | tf_op jit(solution)/shard_map/all_gather | solution.py:104
  7.9 161.1 %all-gather.9.cloned.1.call-start = ((), (), s32[]{:S(2)}) async-start(), calls=%async_computation.7 | async-start | bytes 1327104 | tf_op jit(solution)/shard_map/all_gather | solution.py:105
  8.7 191.5 %all-gather.11.cloned.1.call-start = ((), (), s32[]{:S(2)}) async-start(), calls=%async_computation.8 | async-start | bytes 5308416 | tf_op jit(solution)/shard_map/all_gather | solution.py:106
  9.4 270.5 %all-gather.13.cloned.1.call-start = ((), (), s32[]{:S(2)}) async-start(), calls=%async_computation.9 | async-start | bytes 5308416 | tf_op jit(solution)/shard_map/all_gather | solution.py:108
  9.4 53.9 %collective-permute-start = (bf16[384]{0:T(512)(128)(2,1)}, bf16[384]{0:T(512)(128)(2,1)S(1)}, u32[]{:S(2)}, u32[]{:S(2)}) collective-permute-start(bf16[384]{0:T(512)(128)(2,1)} %param.21), channel_id=1, source_target_pairs={{0,28},{4,0},{8,4},{12,8},{16,12},{20,16},{24,20},{28,24},{1,29},{... | collective-permute-start | bytes 2312 | tf_op jit(solution)/shard_map/ppermute | solution.py:18
  15.5 562.3 %reduce-scatter.13.cloned.1.call-start = ((), (), s32[]{:S(2)}) async-start(), calls=%async_computation.11 | async-start | bytes 2654208 | tf_op jit(solution)/shard_map/reduce_scatter | solution.py:210
  62.1 22.1 %copy-start.38 = (f32[1024]{0:T(1024)}, f32[1024]{0:T(1024)S(1)}, u32[]{:S(2)}) copy-start(f32[1024]{0:T(1024)S(1)} %broadcast_multiply_fusion.1) | copy-start | bytes 12292
  63.4 3.6 collective-permute-start.1
  67.0 5.1 collective-permute-start.2
  91.9 77.0 %copy-start.57 = (f32[768]{0:T(1024)S(1)}, f32[768]{0:T(1024)}, u32[]{:S(2)}) copy-start(f32[768]{0:T(1024)} %get-tuple-element.272) | copy-start | bytes 9220
  172.9 27.2 %copy-start.32 = (f32[768]{0:T(1024)S(1)}, f32[768]{0:T(1024)}, u32[]{:S(2)}) copy-start(f32[768]{0:T(1024)} %get-tuple-element.276) | copy-start | bytes 9220
  172.9 27.2 %copy-start.36 = (f32[768]{0:T(1024)S(1)}, f32[768]{0:T(1024)}, u32[]{:S(2)}) copy-start(f32[768]{0:T(1024)} %get-tuple-element.270) | copy-start | bytes 9220
  172.9 140.5 %copy-start.29 = (f32[1024]{0:T(1024)}, f32[1024]{0:T(1024)S(1)}, u32[]{:S(2)}) copy-start(f32[1024]{0:T(1024)S(1)} %broadcast_multiply_fusion) | copy-start | bytes 12292
  174.9 138.5 %copy-start.34 = (f32[1024]{0:T(1024)}, f32[1024]{0:T(1024)S(1)}, u32[]{:S(2)}) copy-start(f32[1024]{0:T(1024)S(1)} %fusion.37) | copy-start | bytes 12292
  200.1 79.8 %copy-start.24 = (bf16[1024,768]{1,0:T(8,128)(2,1)S(1)}, bf16[1024,768]{1,0:T(8,128)(2,1)}, u32[]{:S(2)}) copy-start(bf16[1024,768]{1,0:T(8,128)(2,1)} %param.23) | copy-start | bytes 4718596
  200.1 79.8 %copy-start.50 = (f32[3072]{0:T(1024)S(1)}, f32[3072]{0:T(1024)}, u32[]{:S(2)}) copy-start(f32[3072]{0:T(1024)} %dynamic-slice_convert_fusion) | copy-start | bytes 36868
  319.7 327.9 %reduce-scatter.11.cloned.1.call-start = ((), (), s32[]{:S(2)}) async-start(), calls=%async_computation.10 | async-start | bytes 7962624 | tf_op jit(solution)/shard_map/reduce_scatter | solution.py:209
  519.5 293.0 %reduce-scatter.17.cloned.1.call-start = ((), (), s32[]{:S(2)}) async-start(), calls=%async_computation.13 | async-start | bytes 10616832 | tf_op jit(solution)/shard_map/reduce_scatter | solution.py:213
  533.8 443.5 %reduce-scatter.15.cloned.1.call-start = ((), (), s32[]{:S(2)}) async-start(), calls=%async_computation.12 | async-start | bytes 10616832 | tf_op jit(solution)/shard_map/reduce_scatter | solution.py:211
  546.2 496.3 %reduce-scatter.19.cloned.1.call-start = ((), (), s32[]{:S(2)}) async-start(), calls=%async_computation.14 | async-start | bytes 442368
  573.5 403.9 %copy-start.13 = (f32[1024,768]{0,1:T(8,128)S(1)}, f32[1024,768]{0,1:T(8,128)}, u32[]{:S(2)}) copy-start(f32[1024,768]{0,1:T(8,128)} %copy-done.10) | copy-start | bytes 9437188
  573.5 403.9 %copy-start.54 = (f32[768]{0:T(1024)S(1)}, f32[768]{0:T(1024)}, u32[]{:S(2)}) copy-start(f32[768]{0:T(1024)} %get-tuple-element.271) | copy-start | bytes 9220
  573.5 533.9 %reduce-scatter.21.cloned.1.call-start = ((), (), s32[]{:S(2)}) async-start(), calls=%async_computation.15 | async-start | bytes 442368
  576.5 607.6 %all-reduce.5.cloned.1.call-start = ((), (), s32[]{:S(2)}) async-start(), calls=%async_computation.16 | async-start | bytes 7077888 | tf_op jit(solution)/shard_map/psum | solution.py:215
  (57 other events, 321.8 us)
Sparse Core Ops, SparseCore 0:
  10.2 67.6 all-gather.6
  80.0 39.8 all-gather.8
  122.1 78.0 all-gather.10
  202.2 77.6 all-gather.12
  319.9 67.9 reduce-scatter.12
  519.6 127.8 reduce-scatter.10
  651.2 161.2 reduce-scatter.16
  816.1 161.2 reduce-scatter.14
  981.2 61.2 reduce-scatter.18
  1046.2 61.2 reduce-scatter.20
  1110.1 73.9 all-reduce.4
